TPU v7x, 32 devices: a whole 2x2x4 slice. The times are simulated.
32 devices in a mesh: fsdp: 2 (over x), ctx: 4 (over z), tp: 4 (over y, core).
Axes of the slice: x: 2, y: 2, z: 4, core: 2. Of those that a mesh axis runs over, the one named last changes fastest.
Arguments:
- tokens: bfloat16 [4, 2048, 1024], P('fsdp', 'ctx'), may hold values from -6 to 6
- segment_ids: int32 [4, 2048], P('fsdp'), may hold values from 0 to 15, never falling along the last dimension, each value on 1 to 1024 neighbouring positions
- attn_gain: bfloat16 [1024], P('fsdp'), may hold values from 0.25 to 1.75
- w_query: bfloat16 [1024, 2048], P('fsdp', 'tp'), may hold values from -0.1875 to 0.1875
- w_key: bfloat16 [1024, 1024], P('fsdp', 'tp'), may hold values from -0.1875 to 0.1875
- w_value: bfloat16 [1024, 1024], P('fsdp', 'tp'), may hold values from -0.1875 to 0.1875
- query_gain: bfloat16 [128], P('fsdp'), may hold values from 0.099609375 to 1.8984375
- key_gain: bfloat16 [128], P('fsdp'), may hold values from 0.099609375 to 1.8984375
- w_out: bfloat16 [2048, 1024], P('tp', 'fsdp'), may hold values from -0.375 to 0.375
- ffn_gain: bfloat16 [1024], P('fsdp'), may hold values from 0.25 to 1.75
- w_gate: bfloat16 [1024, 3072], P('fsdp', 'tp'), may hold values from -0.1875 to 0.1875
- w_up: bfloat16 [1024, 3072], P('fsdp', 'tp'), may hold values from -0.1875 to 0.1875
- w_down: bfloat16 [3072, 1024], P('tp', 'fsdp'), may hold values from -0.21875 to 0.21875
- out_grad: bfloat16 [4, 2048, 1024], P('fsdp', 'ctx'), may hold values from -6 to 6
Outputs:
- layer_out: bfloat16 [4, 2048, 1024], P('fsdp', 'ctx')
- input_grad: float32 [4, 2048, 1024], P('fsdp', 'ctx')
- attn_gain_grad: float32 [1024], P('fsdp')
- w_query_grad: float32 [1024, 2048], P('fsdp', 'tp')
- w_key_grad: float32 [1024, 1024], P('fsdp', 'tp')
- w_value_grad: float32 [1024, 1024], P('fsdp', 'tp')
- query_gain_grad: float32 [128], P('fsdp')
- key_gain_grad: float32 [128], P('fsdp')
- w_out_grad: float32 [2048, 1024], P('tp', 'fsdp')
- ffn_gain_grad: float32 [1024], P('fsdp')
- w_gate_grad: float32 [1024, 3072], P('fsdp', 'tp')
- w_up_grad: float32 [1024, 3072], P('fsdp', 'tp')
- w_down_grad: float32 [3072, 1024], P('tp', 'fsdp')
Inputs may be any that keep to these rules, and one draw needn't show every extreme that they name: `segment_ids`: ids never fall along a sequence, every id of 0 to 15 occurs in each sequence (so the padding segment 0 comes first), a segment has 1 to 1024 positions and some segment exactly 1024.
All inputs are finite; a program needn't handle non-finite values.
Results may differ from a plain program's by a relative error of at most 0.025.
Values may be sent and summed in bfloat16 or wider, within the bound.
No kernel may reach another device: no remote copies, remote signals or barrier semaphores. Data moves between devices by JAX's collectives and lax.ppermute only.
A program may use at most 192 MiB of HBM per device.

v0:
```python
import jax
import jax.numpy as jnp
from jax import lax
from jax.sharding import PartitionSpec as P

epsilon = 1e-06
rope_base = 1000000.0
masked_score = -1e30


def rotate(values, cosine, sine):
    half_size = values.shape[-1] // 2
    first = values[..., :half_size]
    second = values[..., half_size:]
    return jnp.concatenate([first * cosine - second * sine, second * cosine + first * sine], -1)


def inv_scale(values):
    return lax.rsqrt(jnp.mean(values * values, -1, keepdims=True) + epsilon)


def norm_back(values, scale, gain, grad):
    scaled = grad * gain
    return scale * scaled - values * scale * scale * scale * jnp.mean(
        scaled * values, -1, keepdims=True
    )


def body(
    tokens,
    segment_ids,
    attn_gain,
    w_query,
    w_key,
    w_value,
    query_gain,
    key_gain,
    w_out,
    ffn_gain,
    w_gate,
    w_up,
    w_down,
    out_grad,
):
    (
        full_attn_gain,
        full_query,
        full_key,
        full_value,
        full_qgain,
        full_kgain,
        full_out,
        full_ffn_gain,
        full_gate,
        full_up,
        full_down,
    ) = (
        lax.all_gather(attn_gain, "fsdp", axis=0, tiled=True),
        lax.all_gather(w_query, "fsdp", axis=0, tiled=True),
        lax.all_gather(w_key, "fsdp", axis=0, tiled=True),
        lax.all_gather(w_value, "fsdp", axis=0, tiled=True),
        lax.all_gather(query_gain, "fsdp", axis=0, tiled=True),
        lax.all_gather(key_gain, "fsdp", axis=0, tiled=True),
        lax.all_gather(w_out, "fsdp", axis=1, tiled=True),
        lax.all_gather(ffn_gain, "fsdp", axis=0, tiled=True),
        lax.all_gather(w_gate, "fsdp", axis=0, tiled=True),
        lax.all_gather(w_up, "fsdp", axis=0, tiled=True),
        lax.all_gather(w_down, "fsdp", axis=1, tiled=True),
    )
    seq_count, local_len, model_width = tokens.shape
    seq_len = segment_ids.shape[1]
    head_size = full_qgain.shape[0]
    kv_local = full_key.shape[1] // head_size
    heads_local = full_query.shape[1] // head_size
    group_size = heads_local // kv_local
    scale_factor = head_size ** (-0.5)
    index_full = jnp.arange(seq_len, dtype=jnp.int32)[None, :]
    previous = jnp.concatenate([segment_ids[:, :1] - 1, segment_ids[:, :-1]], 1)
    starts = jnp.where(segment_ids != previous, index_full, 0)
    position_full = index_full - lax.cummax(starts, axis=1)
    offset = lax.axis_index("ctx") * local_len
    query_index = offset + jnp.arange(local_len, dtype=jnp.int32)
    query_seg = lax.dynamic_slice_in_dim(segment_ids, offset, local_len, 1)
    query_pos = lax.dynamic_slice_in_dim(position_full, offset, local_len, 1)
    valid = (query_seg != 0).astype(jnp.float32)
    valid_three = valid[:, :, None]
    half_size = head_size // 2
    frequency = rope_base ** (-(jnp.arange(half_size, dtype=jnp.float32) * 2.0 / head_size))
    turned = query_pos.astype(jnp.float32)[:, :, None] * frequency
    cosine = jnp.cos(turned)[:, :, None, :]
    sine = jnp.sin(turned)[:, :, None, :]
    tokens_f = tokens.astype(jnp.float32)
    gain_one = full_attn_gain.astype(jnp.float32)
    gain_two = full_ffn_gain.astype(jnp.float32)
    qgain = full_qgain.astype(jnp.float32)
    kgain = full_kgain.astype(jnp.float32)
    attn_scale = inv_scale(tokens_f)
    normed = (tokens_f * attn_scale * gain_one).astype(jnp.bfloat16)
    query_pre = jnp.einsum(
        "bsd,dh->bsh", normed, full_query, preferred_element_type=jnp.float32
    ).reshape(seq_count, local_len, heads_local, head_size)
    key_pre = jnp.einsum(
        "bsd,dh->bsh", normed, full_key, preferred_element_type=jnp.float32
    ).reshape(seq_count, local_len, kv_local, head_size)
    value_pre = jnp.einsum("bsd,dh->bsh", normed, full_value, preferred_element_type=jnp.float32)
    query_scale = inv_scale(query_pre)
    key_scale = inv_scale(key_pre)
    queries = (
        rotate(query_pre * query_scale * qgain, cosine, sine)
        .astype(jnp.bfloat16)
        .reshape(seq_count, local_len, kv_local, group_size, head_size)
    )
    keys = rotate(key_pre * key_scale * kgain, cosine, sine).astype(jnp.bfloat16)
    values = value_pre.astype(jnp.bfloat16).reshape(seq_count, local_len, kv_local, head_size)

    def allowed_mask(count):
        key_index = jnp.arange(count, dtype=jnp.int32)
        joined = (
            (query_seg[:, :, None] == segment_ids[:, None, :])
            & (key_index[None, None, :] <= query_index[None, :, None])
            & (segment_ids[:, None, :] != 0)
        )
        return joined[:, :, None, None, :]

    stat_shape = (seq_count, local_len, kv_local, group_size)
    run_max = jnp.full(stat_shape, masked_score, jnp.float32)
    piece_keys = lax.all_gather(keys, "ctx", axis=1, tiled=True)
    piece_values = lax.all_gather(values, "ctx", axis=1, tiled=True)
    allowed = allowed_mask(piece_keys.shape[1])
    scores = (
        jnp.einsum("bqkgd,btkd->bqkgt", queries, piece_keys, preferred_element_type=jnp.float32)
        * scale_factor
    )
    masked = jnp.where(allowed, scores, masked_score)
    new_max = jnp.maximum(run_max, jnp.max(masked, -1))
    weights = jnp.where(allowed, jnp.exp(masked - new_max[..., None]), 0.0)
    new_total = jnp.sum(weights, -1)
    new_acc = jnp.einsum(
        "bqkgt,btkd->bqkgd",
        weights.astype(jnp.bfloat16),
        piece_values,
        preferred_element_type=jnp.float32,
    )
    total_safe = jnp.where(query_seg[:, :, None, None] != 0, new_total, 1.0)
    mixed = new_acc / total_safe[..., None] * valid[:, :, None, None, None]
    log_total = new_max + jnp.log(total_safe)
    mixed_low = mixed.astype(jnp.bfloat16)
    out_four = full_out.reshape(kv_local, group_size, head_size, model_width)
    branch_part = jnp.einsum(
        "bqkgd,kgde->bqe", mixed_low, out_four, preferred_element_type=jnp.float32
    )
    branch = lax.psum(branch_part.astype(jnp.bfloat16), "tp").astype(jnp.float32)
    resid = tokens_f + valid_three * branch
    ffn_scale = inv_scale(resid)
    normed_two = (resid * ffn_scale * gain_two).astype(jnp.bfloat16)
    gate = jnp.einsum("bsd,df->bsf", normed_two, full_gate, preferred_element_type=jnp.float32)
    upper = jnp.einsum("bsd,df->bsf", normed_two, full_up, preferred_element_type=jnp.float32)
    sigma = jax.nn.sigmoid(gate)
    silu_gate = gate * sigma
    active = (silu_gate * upper).astype(jnp.bfloat16)
    ffn_part = jnp.einsum("bsf,fd->bsd", active, full_down, preferred_element_type=jnp.float32)
    ffn_out = lax.psum(ffn_part.astype(jnp.bfloat16), "tp").astype(jnp.float32)
    layer_out = (resid + valid_three * ffn_out).astype(jnp.bfloat16)
    back_query, back_key, back_value, back_out, back_gate, back_up, back_down = (
        lax.all_gather(w_query, "fsdp", axis=0, tiled=True),
        lax.all_gather(w_key, "fsdp", axis=0, tiled=True),
        lax.all_gather(w_value, "fsdp", axis=0, tiled=True),
        lax.all_gather(w_out, "fsdp", axis=1, tiled=True),
        lax.all_gather(w_gate, "fsdp", axis=0, tiled=True),
        lax.all_gather(w_up, "fsdp", axis=0, tiled=True),
        lax.all_gather(w_down, "fsdp", axis=1, tiled=True),
    )
    grad_f = out_grad.astype(jnp.float32)
    grad_branch_two = (valid_three * grad_f).astype(jnp.bfloat16)
    down_grad = jnp.einsum(
        "bsf,bsd->fd", active, grad_branch_two, preferred_element_type=jnp.float32
    )
    grad_active = jnp.einsum(
        "bsd,fd->bsf", grad_branch_two, back_down, preferred_element_type=jnp.float32
    )
    grad_gate = (grad_active * upper * sigma * (1.0 + gate * (1.0 - sigma))).astype(jnp.bfloat16)
    grad_upper = (grad_active * silu_gate).astype(jnp.bfloat16)
    gate_grad = jnp.einsum("bsd,bsf->df", normed_two, grad_gate, preferred_element_type=jnp.float32)
    up_grad = jnp.einsum("bsd,bsf->df", normed_two, grad_upper, preferred_element_type=jnp.float32)
    grad_two_part = jnp.einsum(
        "bsf,df->bsd", grad_gate, back_gate, preferred_element_type=jnp.float32
    ) + jnp.einsum("bsf,df->bsd", grad_upper, back_up, preferred_element_type=jnp.float32)
    grad_two = lax.psum(grad_two_part.astype(jnp.bfloat16), "tp").astype(jnp.float32)
    ffn_gain_grad = jnp.sum(grad_two * resid * ffn_scale, (0, 1))
    grad_resid = grad_f + norm_back(resid, ffn_scale, gain_two, grad_two)
    grad_branch = (valid_three * grad_resid).astype(jnp.bfloat16)
    out_weight_grad = jnp.einsum(
        "bqkgd,bqe->kgde", mixed_low, grad_branch, preferred_element_type=jnp.float32
    ).reshape(heads_local * head_size, model_width)
    back_four = back_out.reshape(kv_local, group_size, head_size, model_width)
    grad_mixed = jnp.einsum(
        "bqe,kgde->bqkgd", grad_branch, back_four, preferred_element_type=jnp.float32
    ).astype(jnp.bfloat16)
    delta = jnp.sum(grad_mixed.astype(jnp.float32) * mixed, -1)
    piece_keys = lax.all_gather(keys, "ctx", axis=1, tiled=True)
    piece_values = lax.all_gather(values, "ctx", axis=1, tiled=True)
    count = piece_keys.shape[1]
    allowed = allowed_mask(count)
    scores = (
        jnp.einsum("bqkgd,btkd->bqkgt", queries, piece_keys, preferred_element_type=jnp.float32)
        * scale_factor
    )
    probs = jnp.where(
        allowed,
        jnp.exp(jnp.where(allowed, scores, 0.0) - jnp.where(allowed, log_total[..., None], 0.0)),
        0.0,
    )
    value_term = jnp.einsum(
        "bqkgt,bqkgd->btkd",
        probs.astype(jnp.bfloat16),
        grad_mixed,
        preferred_element_type=jnp.float32,
    )
    grad_probs = jnp.einsum(
        "bqkgd,btkd->bqkgt", grad_mixed, piece_values, preferred_element_type=jnp.float32
    )
    grad_scores = (probs * (grad_probs - delta[..., None])).astype(jnp.bfloat16)
    query_term = (
        jnp.einsum("bqkgt,btkd->bqkgd", grad_scores, piece_keys, preferred_element_type=jnp.float32)
        * scale_factor
    )
    key_term = (
        jnp.einsum("bqkgt,bqkgd->btkd", grad_scores, queries, preferred_element_type=jnp.float32)
        * scale_factor
    )
    key_full = key_term
    value_full = value_term
    grad_query_rot, key_full, value_full = (query_term, key_full, value_full)
    grad_key_rot, grad_value = (
        lax.psum_scatter(
            key_full.astype(jnp.bfloat16), "ctx", scatter_dimension=1, tiled=True
        ).astype(jnp.float32),
        lax.psum_scatter(
            value_full.astype(jnp.bfloat16), "ctx", scatter_dimension=1, tiled=True
        ).astype(jnp.float32),
    )
    grad_query_norm = rotate(
        grad_query_rot.reshape(seq_count, local_len, heads_local, head_size), cosine, -sine
    )
    grad_key_norm = rotate(grad_key_rot, cosine, -sine)
    qgain_part = jnp.sum(grad_query_norm * query_pre * query_scale, (0, 1, 2))
    kgain_part = jnp.sum(grad_key_norm * key_pre * key_scale, (0, 1, 2))
    grad_query_pre = (
        norm_back(query_pre, query_scale, qgain, grad_query_norm)
        .astype(jnp.bfloat16)
        .reshape(seq_count, local_len, heads_local * head_size)
    )
    grad_key_pre = (
        norm_back(key_pre, key_scale, kgain, grad_key_norm)
        .astype(jnp.bfloat16)
        .reshape(seq_count, local_len, kv_local * head_size)
    )
    grad_value_pre = grad_value.astype(jnp.bfloat16).reshape(
        seq_count, local_len, kv_local * head_size
    )
    query_grad = jnp.einsum(
        "bsd,bsh->dh", normed, grad_query_pre, preferred_element_type=jnp.float32
    )
    key_grad = jnp.einsum("bsd,bsh->dh", normed, grad_key_pre, preferred_element_type=jnp.float32)
    value_grad = jnp.einsum(
        "bsd,bsh->dh", normed, grad_value_pre, preferred_element_type=jnp.float32
    )
    grad_one_part = (
        jnp.einsum("bsh,dh->bsd", grad_query_pre, back_query, preferred_element_type=jnp.float32)
        + jnp.einsum("bsh,dh->bsd", grad_key_pre, back_key, preferred_element_type=jnp.float32)
        + jnp.einsum("bsh,dh->bsd", grad_value_pre, back_value, preferred_element_type=jnp.float32)
    )
    grad_one, qgain_grad, kgain_grad = (
        lax.psum(grad_one_part.astype(jnp.bfloat16), "tp").astype(jnp.float32),
        lax.psum(qgain_part.astype(jnp.bfloat16), "tp").astype(jnp.float32),
        lax.psum(kgain_part.astype(jnp.bfloat16), "tp").astype(jnp.float32),
    )
    attn_gain_grad = jnp.sum(grad_one * tokens_f * attn_scale, (0, 1))
    input_grad = grad_resid + norm_back(tokens_f, attn_scale, gain_one, grad_one)
    reduced = (
        lax.psum_scatter(
            attn_gain_grad.astype(jnp.bfloat16), "fsdp", scatter_dimension=0, tiled=True
        ).astype(jnp.float32),
        lax.psum_scatter(
            query_grad.astype(jnp.bfloat16), "fsdp", scatter_dimension=0, tiled=True
        ).astype(jnp.float32),
        lax.psum_scatter(
            key_grad.astype(jnp.bfloat16), "fsdp", scatter_dimension=0, tiled=True
        ).astype(jnp.float32),
        lax.psum_scatter(
            value_grad.astype(jnp.bfloat16), "fsdp", scatter_dimension=0, tiled=True
        ).astype(jnp.float32),
        lax.psum_scatter(
            qgain_grad.astype(jnp.bfloat16), "fsdp", scatter_dimension=0, tiled=True
        ).astype(jnp.float32),
        lax.psum_scatter(
            kgain_grad.astype(jnp.bfloat16), "fsdp", scatter_dimension=0, tiled=True
        ).astype(jnp.float32),
        lax.psum_scatter(
            out_weight_grad.astype(jnp.bfloat16), "fsdp", scatter_dimension=1, tiled=True
        ).astype(jnp.float32),
        lax.psum_scatter(
            ffn_gain_grad.astype(jnp.bfloat16), "fsdp", scatter_dimension=0, tiled=True
        ).astype(jnp.float32),
        lax.psum_scatter(
            gate_grad.astype(jnp.bfloat16), "fsdp", scatter_dimension=0, tiled=True
        ).astype(jnp.float32),
        lax.psum_scatter(
            up_grad.astype(jnp.bfloat16), "fsdp", scatter_dimension=0, tiled=True
        ).astype(jnp.float32),
        lax.psum_scatter(
            down_grad.astype(jnp.bfloat16), "fsdp", scatter_dimension=1, tiled=True
        ).astype(jnp.float32),
    )
    summed = (
        lax.psum(reduced[0].astype(jnp.bfloat16), "ctx").astype(jnp.float32),
        lax.psum(reduced[1].astype(jnp.bfloat16), "ctx").astype(jnp.float32),
        lax.psum(reduced[2].astype(jnp.bfloat16), "ctx").astype(jnp.float32),
        lax.psum(reduced[3].astype(jnp.bfloat16), "ctx").astype(jnp.float32),
        lax.psum(reduced[4].astype(jnp.bfloat16), "ctx").astype(jnp.float32),
        lax.psum(reduced[5].astype(jnp.bfloat16), "ctx").astype(jnp.float32),
        lax.psum(reduced[6].astype(jnp.bfloat16), "ctx").astype(jnp.float32),
        lax.psum(reduced[7].astype(jnp.bfloat16), "ctx").astype(jnp.float32),
        lax.psum(reduced[8].astype(jnp.bfloat16), "ctx").astype(jnp.float32),
        lax.psum(reduced[9].astype(jnp.bfloat16), "ctx").astype(jnp.float32),
        lax.psum(reduced[10].astype(jnp.bfloat16), "ctx").astype(jnp.float32),
    )
    return (
        layer_out,
        input_grad,
        summed[0],
        summed[1],
        summed[2],
        summed[3],
        summed[4],
        summed[5],
        summed[6],
        summed[7],
        summed[8],
        summed[9],
        summed[10],
    )


def solution(mesh):
    placed = (
        P("fsdp", "ctx", None),
        P("fsdp", None),
        P("fsdp"),
        P("fsdp", "tp"),
        P("fsdp", "tp"),
        P("fsdp", "tp"),
        P("fsdp"),
        P("fsdp"),
        P("tp", "fsdp"),
        P("fsdp"),
        P("fsdp", "tp"),
        P("fsdp", "tp"),
        P("tp", "fsdp"),
        P("fsdp", "ctx", None),
    )
    return jax.shard_map(
        body,
        mesh=mesh,
        in_specs=placed,
        out_specs=(
            P("fsdp", "ctx", None),
            P("fsdp", "ctx", None),
            P("fsdp"),
            P("fsdp", "tp"),
            P("fsdp", "tp"),
            P("fsdp", "tp"),
            P("fsdp"),
            P("fsdp"),
            P("tp", "fsdp"),
            P("fsdp"),
            P("fsdp", "tp"),
            P("fsdp", "tp"),
            P("tp", "fsdp"),
        ),
        check_vma=False,
    )
```

profile of v0, /device:TPU:0, one launch (start us, length us, event | category | flops | bytes accessed | tf_op | source)
XLA Modules:
  0.0 928.1 jit_solution(4689510979285144952)
XLA Ops:
  10.2 5.3 all-gather
  17.8 13.3 %all_gather.51 = bf16[1024,256]{0,1:T(8,128)(2,1)S(1)} all-gather(bf16[512,256]{0,1:T(8,128)(2,1)S(1)} %copy.220), channel_id=1, replica_groups=mesh['fsdp'=2,'ctx'=4,'tp'=4] {'fsdp'}, dimensions={0}, use_global_device_ids=true | all-gather | bytes 786432 | tf_op jit(solution)/shard_map/all_gather | solution.py:60
  39.6 5.4 all-reduce.11
  52.8 7.1 all_gather.49
  63.8 4.2 and_and_fusion
  74.9 24.4 %all-gather.12.cloned.1.call-done = bf16[2,2048,2,128]{3,1,2,0:T(8,128)(2,1)} async-done(((bf16[2,512,2,128]{3,1,2,0:T(8,128)(2,1)}), bf16[2,2048,2,128]{3,1,2,0:T(8,128)(2,1)}) %all-gather.12.cloned.1.call-update) | async-done | bytes 2097168 | tf_op jit(solution)/shard_map/all_gather | solution.py:127
  99.3 16.5 %fusion.5 = (f32[2,512,2,2]{1,3,2,0:T(2,128)S(1)}, f32[2,2,2048,512,2]{3,2,4,1,0:T(8,128)}) fusion(pred[2,512,2048]{1,2,0:T(8,128)(4,1)} %and_and_fusion, bf16[2,512,2,2,64]{4,1,3,2,0:T(8,128)(2,1)} %bitcast.292, bf16[2,512,2,2,64]{4,1,3,2,0:T(8,128)(2,1)} %bitcast.290, bf16[2,2048,2,128]{3,1,2,0:T(8,128)(2,1)} %all-gather.12.cloned.1.call-done), kind=kOutput, calls=%fused_computation.9 | convolution fusion | flops 2174742528 | bytes 38813696 | tf_op jit(solution)/shard_map/bqkgd,btkd->bqkgt/dot_general | solution.py:131
  115.8 15.0 %fusion.6 = f32[2,512,2,2]{1,3,2,0:T(2,128)S(1)} fusion(f32[2,2,2048,512,2]{3,2,4,1,0:T(8,128)} %get-tuple-element.74, f32[2,512,2,2]{1,3,2,0:T(2,128)S(1)} %broadcast_maximum_fusion, pred[2,512,2048]{1,2,0:T(8,128)(4,1)S(1)} %copy-done.7), kind=kLoop, calls=%fused_computation.10 | loop fusion | flops 41938944 | bytes 35684352 | tf_op jit(solution)/shard_map/reduce_sum | solution.py:137
  130.9 15.0 %all-gather.10.cloned.1.call-done = bf16[2,2048,2,128]{1,3,2,0:T(8,128)(2,1)} async-done(((bf16[2,512,2,128]{1,3,2,0:T(8,128)(2,1)}), bf16[2,2048,2,128]{1,3,2,0:T(8,128)(2,1)}) %all-gather.10.cloned.1.call-update) | async-done | bytes 2097168 | tf_op jit(solution)/shard_map/all_gather | solution.py:128
  145.9 18.1 %fusion.114 = (bf16[2,512,2,2,128]{1,4,3,2,0:T(8,128)(2,1)S(1)}, f32[2,512,2,2,128]{1,4,3,2,0:T(8,128)}) fusion(f32[2,512]{1,0:T(2,128)S(1)} %get-tuple-element.42, f32[2,512,2,2]{1,3,2,0:T(2,128)S(1)} %get-tuple-element.41, f32[2,2,2048,512,2]{3,2,4,1,0:T(8,128)} %get-tuple-element.74, f32[2,512,2,2]{1,3,2,0:T(2,128)S(1)} %broadcast_maximum_fusion, ...), kind=kOutput, calls=%fused_computation.193 | convolution fusion | flops 2190999552 | bytes 40931328 | tf_op jit(solution)/shard_map/bqkgt,btkd->bqkgd/dot_general | solution.py:138
  164.0 3.4 all-gather.16.cloned.1.call-done
  167.4 3.8 bitcast_convert_fusion
  173.5 4.4 all-gather.1
  177.8 45.0 %all-reduce.17.cloned.1.call-done = bf16[2,512,1024]{2,1,0:T(8,128)(2,1)} async-done(((bf16[2,512,1024]{2,1,0:T(8,128)(2,1)}), bf16[2,512,1024]{2,1,0:T(8,128)(2,1)}) %all-reduce.17.cloned.1.call-update) | async-done | bytes 2097168 | tf_op jit(solution)/shard_map/psum | solution.py:152
  227.9 23.7 %all-gather.20.cloned.1.call-done = bf16[1024,768]{1,0:T(8,128)(2,1)} async-done(((bf16[512,768]{1,0:T(8,128)(2,1)}), bf16[1024,768]{1,0:T(8,128)(2,1)}) %all-gather.20.cloned.1.call-update) | async-done | bytes 1572880 | tf_op jit(solution)/shard_map/all_gather | solution.py:67
  251.5 5.5 fusion.70
  257.0 23.3 %all-gather.18.cloned.1.call-done = bf16[1024,768]{1,0:T(8,128)(2,1)} async-done(((bf16[512,768]{1,0:T(8,128)(2,1)}), bf16[1024,768]{1,0:T(8,128)(2,1)}) %all-gather.18.cloned.1.call-update) | async-done | bytes 1572880 | tf_op jit(solution)/shard_map/all_gather | solution.py:66
  280.3 5.5 fusion.74
  285.8 23.3 %all-gather.22.cloned.1.call-done = bf16[768,1024]{1,0:T(8,128)(2,1)} async-done(((bf16[768,512]{1,0:T(8,128)(2,1)}), bf16[768,1024]{1,0:T(8,128)(2,1)}) %all-gather.22.cloned.1.call-update) | async-done | bytes 1572880 | tf_op jit(solution)/shard_map/all_gather | solution.py:68
  309.0 8.0 multiply_convert_fusion.2
  319.6 3.2 add_convert_fusion.1
  322.8 51.5 %all-reduce.19.cloned.1.call-done = bf16[2,512,1024]{2,1,0:T(8,128)(2,1)} async-done(((bf16[2,512,1024]{2,1,0:T(8,128)(2,1)}), bf16[2,512,1024]{2,1,0:T(8,128)(2,1)}) %all-reduce.19.cloned.1.call-update) | async-done | bytes 2097168 | tf_op jit(solution)/shard_map/psum | solution.py:188
  374.3 4.2 fusion.29
  378.7 4.5 multiply_reduce_fusion.2
  384.1 21.8 %fusion.1 = bf16[2,512,2,2,2048]{1,4,3,2,0:T(8,128)(2,1)} fusion(f32[2,2,2048,512,2]{3,2,4,1,0:T(8,128)} %get-tuple-element.74, f32[2,512,2,2]{1,3,2,0:T(2,128)S(1)} %get-tuple-element.77, f32[2,512,2,2]{1,3,2,0:T(2,128)S(1)} %get-tuple-element.40, pred[2,512,2048]{1,2,0:T(8,128)(4,1)S(1)} %copy-done.8, ...), kind=kOutput, calls=%fused_computation.2 | convolution fusion | flops 2214592512 | bytes 55607296 | tf_op jit(solution)/shard_map/bqkgd,btkd->bqkgt/dot_general | solution.py:219
  406.0 11.7 %fusion.38 = bf16[2,2048,2,128]{3,1,2,0:T(8,128)(2,1)} fusion(bf16[2,512,2,2,2048]{1,4,3,2,0:T(8,128)(2,1)} %fusion.1, bf16[2,512,2,2,64]{4,1,3,2,0:T(8,128)(2,1)S(1)} %bitcast.293, bf16[2,512,2,2,64]{4,1,3,2,0:T(8,128)(2,1)S(1)} %bitcast.291), kind=kOutput, calls=%fused_computation.76 | convolution fusion | flops 2151677952 | bytes 19922944 | tf_op jit(solution)/shard_map/bqkgt,bqkgd->btkd/dot_general | solution.py:228
  417.8 19.0 %fusion.39 = bf16[2,2048,2,128]{1,3,2,0:T(8,128)(2,1)} fusion(bf16[2,512,2,2,128]{1,4,3,2,0:T(8,128)(2,1)} %copy-done.57, f32[2,2,2048,512,2]{3,2,4,1,0:T(8,128)} %get-tuple-element.74, f32[2,512,2,2]{1,3,2,0:T(2,128)S(1)} %get-tuple-element.40, pred[2,512,2048]{1,2,0:T(8,128)(4,1)} %and_and_fusion), kind=kOutput, calls=%fused_computation.77 | convolution fusion | flops 2198863872 | bytes 38813696 | tf_op jit(solution)/shard_map/bqkgt,bqkgd->btkd/dot_general | solution.py:213
  436.9 5.5 fusion.46
  443.6 5.1 bitcast_convert_fusion.4
  448.8 5.0 bitcast_convert_fusion.3
  454.1 9.1 fusion.64
  470.0 5.2 bitcast_convert_fusion.2
  486.8 5.1 convolution_convert_fusion
  491.8 15.5 %reduce-scatter.12.cloned.1.call-done = bf16[2,512,2,128]{1,3,2,0:T(8,128)(2,1)} async-done(((bf16[2,2048,2,128]{1,3,2,0:T(8,128)(2,1)}), bf16[2,512,2,128]{1,3,2,0:T(8,128)(2,1)}) %reduce-scatter.12.cloned.1.call-update) | async-done | bytes 524304 | tf_op jit(solution)/shard_map/reduce_scatter | solution.py:238
  516.4 12.6 %reduce-scatter.20.cloned.1.call-done = bf16[512,512]{1,0:T(8,128)(2,1)} async-done(((bf16[512,1024]{1,0:T(8,128)(2,1)}), bf16[512,512]{1,0:T(8,128)(2,1)}) %reduce-scatter.20.cloned.1.call-update) | async-done | bytes 524304 | tf_op jit(solution)/shard_map/reduce_scatter | solution.py:299
  529.0 29.0 %reduce-scatter.22.cloned.1.call-done = bf16[512,768]{1,0:T(8,128)(2,1)} async-done(((bf16[1024,768]{1,0:T(8,128)(2,1)}), bf16[512,768]{1,0:T(8,128)(2,1)}) %reduce-scatter.22.cloned.1.call-update) | async-done | bytes 786448 | tf_op jit(solution)/shard_map/reduce_scatter | solution.py:305
  558.0 28.9 %reduce-scatter.24.cloned.1.call-done = bf16[512,768]{1,0:T(8,128)(2,1)} async-done(((bf16[1024,768]{1,0:T(8,128)(2,1)}), bf16[512,768]{1,0:T(8,128)(2,1)}) %reduce-scatter.24.cloned.1.call-update) | async-done | bytes 786448 | tf_op jit(solution)/shard_map/reduce_scatter | solution.py:308
  586.9 22.5 %reduce-scatter.14.cloned.1.call-done = bf16[512,512]{1,0:T(8,128)(2,1)} async-done(((bf16[1024,512]{1,0:T(8,128)(2,1)}), bf16[512,512]{1,0:T(8,128)(2,1)}) %reduce-scatter.14.cloned.1.call-update) | async-done | bytes 524304 | tf_op jit(solution)/shard_map/reduce_scatter | solution.py:284
  609.4 28.3 %reduce-scatter.26.cloned.1.call-done = bf16[768,512]{1,0:T(8,128)(2,1)} async-done(((bf16[768,1024]{1,0:T(8,128)(2,1)}), bf16[768,512]{1,0:T(8,128)(2,1)}) %reduce-scatter.26.cloned.1.call-update) | async-done | bytes 786448 | tf_op jit(solution)/shard_map/reduce_scatter | solution.py:311
  637.7 17.3 %reduce-scatter.16.cloned.1.call-done = bf16[512,256]{1,0:T(8,128)(2,1)} async-done(((bf16[1024,256]{1,0:T(8,128)(2,1)}), bf16[512,256]{1,0:T(8,128)(2,1)}) %reduce-scatter.16.cloned.1.call-update) | async-done | bytes 262160 | tf_op jit(solution)/shard_map/reduce_scatter | solution.py:287
  655.0 17.3 %reduce-scatter.18.cloned.1.call-done = bf16[512,256]{1,0:T(8,128)(2,1)} async-done(((bf16[1024,256]{1,0:T(8,128)(2,1)}), bf16[512,256]{1,0:T(8,128)(2,1)}) %reduce-scatter.18.cloned.1.call-update) | async-done | bytes 262160 | tf_op jit(solution)/shard_map/reduce_scatter | solution.py:290
  673.7 87.2 %all-reduce.21.cloned.1.call-done = (bf16[2,512,1024]{2,1,0:T(8,128)(2,1)}, bf16[2,512,1024]{2,1,0:T(8,128)(2,1)}) async-done(((bf16[2,512,1024]{2,1,0:T(8,128)(2,1)}, bf16[2,512,1024]{2,1,0:T(8,128)(2,1)}), (bf16[2,512,1024]{2,1,0:T(8,128)(2,1)}, bf16[2,512,1024]{2,1,0:T(8,128)(2,1)})) %all-reduce.21.cloned.1.call-update) | async-done | bytes 4194320 | tf_op jit(solution)/shard_map/psum | solution.py:162
  760.9 3.4 fusion.33
  764.4 5.0 all-reduce.10
  769.7 6.0 all-reduce.6
  775.7 12.3 %all-reduce.8 = (bf16[512]{0:T(512)(128)(2,1)S(1)}, bf16[64]{0:T(256)(128)(2,1)S(1)}, bf16[64]{0:T(256)(128)(2,1)S(1)}, bf16[512]{0:T(512)(128)(2,1)S(1)}) all-reduce(bf16[512]{0:T(512)(128)(2,1)S(1)} %dynamic-slice.3, bf16[64]{0:T(256)(128)(2,1)S(1)} %get-tuple-element.17, ...), channel_id=1, replica_groups=mesh['fsdp'=2,'ctx'=4,'tp'=4] {'ctx'}, use_global_device_ids=true, to_apply=%region_21.22 | all-reduce | flops 1152 | bytes 4608 | tf_op jit(solution)/shard_map/psum | solution.py:316
  790.2 8.0 fusion.24
  798.2 112.6 %all-reduce.23.cloned.1.call-done = (bf16[512,512]{1,0:T(8,128)(2,1)}, bf16[512,256]{1,0:T(8,128)(2,1)}, bf16[512,256]{1,0:T(8,128)(2,1)}, bf16[512,512]{1,0:T(8...) async-done(((bf16[512,512]{1,0:T(8,128)(2,1)}, bf16[512,256]{1,0:T(8,128)(2,1)}, bf16[512,256]{1,0:T(8,128)(2,1)}, ...) | async-done | bytes 3932176 | tf_op jit(solution)/shard_map/psum | solution.py:317
  (249 shorter events, 83.7 us)
Async XLA Ops:
  7.2 25.1 %copy-start = (bf16[2,512,1024]{2,1,0:T(8,128)(2,1)S(1)}, bf16[2,512,1024]{2,1,0:T(8,128)(2,1)}, u32[]{:S(2)}) copy-start(bf16[2,512,1024]{2,1,0:T(8,128)(2,1)} %param.14) | copy-start | bytes 6291460
  7.2 10.4 %copy-start.32 = (bf16[512,256]{1,0:T(8,128)(2,1)S(1)}, bf16[512,256]{1,0:T(8,128)(2,1)}, u32[]{:S(2)}) copy-start(bf16[512,256]{1,0:T(8,128)(2,1)} %param.18) | copy-start | bytes 786436
  7.2 23.9 %copy-start.29 = (s32[2,2048]{1,0:T(2,128)S(1)}, s32[2,2048]{1,0:T(2,128)}, u32[]{:S(2)}) copy-start(s32[2,2048]{1,0:T(2,128)} %param.15) | copy-start | bytes 49156
  7.2 60.8 %all-gather.14.cloned.1.call-start = ((), (), s32[]{:S(2)}) async-start(), calls=%async_computation.11 | async-start | bytes 1572864 | tf_op jit(solution)/shard_map/all_gather | solution.py:59
  9.5 89.8 %all-gather.12.cloned.1.call-start = ((), (), s32[]{:S(2)}) async-start(), calls=%async_computation.10 | async-start | bytes 2621440 | tf_op jit(solution)/shard_map/all_gather | solution.py:127
  15.5 52.5 %copy-start.37 = (f32[2,1,512]{2,1,0:T(1,128)}, f32[2,1,512]{2,1,0:T(1,128)S(1)}, u32[]{:S(2)}) copy-start(f32[2,1,512]{2,1,0:T(1,128)S(1)} %convert_element_type.277) | copy-start | bytes 12292
  17.6 50.4 %copy-start.39 = (f32[2,512]{1,0:T(2,128)}, f32[2,512]{1,0:T(2,128)S(1)}, u32[]{:S(2)}) copy-start(f32[2,512]{1,0:T(2,128)S(1)} %add_rsqrt_fusion.3) | copy-start | bytes 12292
  31.1 4.9 copy-start.16
  32.3 5.4 copy-start.45
  32.3 6.8 copy-start.51
  32.3 7.0 copy-start.52
  36.0 35.2 %copy-start.10 = (f32[2,512,64]{1,2,0:T(8,128)}, f32[2,512,64]{1,2,0:T(8,128)S(1)}, u32[]{:S(2)}) copy-start(f32[2,512,64]{1,2,0:T(8,128)S(1)} %get-tuple-element.66) | copy-start | bytes 786436
  37.7 12.8 %copy-start.5 = (f32[2,512,2,128]{3,1,2,0:T(8,128)}, f32[2,512,2,128]{3,1,2,0:T(8,128)S(1)}, u32[]{:S(2)}) copy-start(f32[2,512,2,128]{3,1,2,0:T(8,128)S(1)} %copy.221) | copy-start | bytes 3145732
  45.0 5.6 copy-start.43
  51.7 94.3 %all-gather.10.cloned.1.call-start = ((), (), s32[]{:S(2)}) async-start(), calls=%async_computation.9 | async-start | bytes 2621440 | tf_op jit(solution)/shard_map/all_gather | solution.py:128
  62.3 105.1 %all-gather.16.cloned.1.call-start = ((), (), s32[]{:S(2)}) async-start(), calls=%async_computation.12 | async-start | bytes 1572864 | tf_op jit(solution)/shard_map/all_gather | solution.py:64
  62.9 160.0 %all-reduce.17.cloned.1.call-start = ((), (), s32[]{:S(2)}) async-start(), calls=%async_computation.13 | async-start | bytes 4194304 | tf_op jit(solution)/shard_map/psum | solution.py:152
  63.0 7.7 copy-start.41
  99.3 16.6 %copy-start.7 = (pred[2,512,2048]{1,2,0:T(8,128)(4,1)S(1)}, pred[2,512,2048]{1,2,0:T(8,128)(4,1)}, u32[]{:S(2)}) copy-start(pred[2,512,2048]{1,2,0:T(8,128)(4,1)} %and_and_fusion) | copy-start | bytes 6291460
  164.0 7.3 copy-start.53
  171.3 80.2 %all-gather.20.cloned.1.call-start = ((), (), s32[]{:S(2)}) async-start(), calls=%async_computation.15 | async-start | bytes 2359296 | tf_op jit(solution)/shard_map/all_gather | solution.py:67
  171.9 108.4 %all-gather.18.cloned.1.call-start = ((), (), s32[]{:S(2)}) async-start(), calls=%async_computation.14 | async-start | bytes 2359296 | tf_op jit(solution)/shard_map/all_gather | solution.py:66
  172.6 136.4 %all-gather.22.cloned.1.call-start = ((), (), s32[]{:S(2)}) async-start(), calls=%async_computation.16 | async-start | bytes 2359296 | tf_op jit(solution)/shard_map/all_gather | solution.py:68
  173.4 200.9 %all-reduce.19.cloned.1.call-start = ((), (), s32[]{:S(2)}) async-start(), calls=%async_computation.17 | async-start | bytes 4194304 | tf_op jit(solution)/shard_map/psum | solution.py:188
  309.0 8.0 copy-start.49
  322.8 55.8 %copy-start.50 = (bf16[512,1024]{1,0:T(8,128)(2,1)S(1)}, bf16[512,1024]{1,0:T(8,128)(2,1)}, u32[]{:S(2)}) copy-start(bf16[512,1024]{1,0:T(8,128)(2,1)} %all-gather.16.cloned.1.call-done) | copy-start | bytes 3145732
  322.8 153.5 %reduce-scatter.10.cloned.1.call-start = ((), (), s32[]{:S(2)}) async-start(), calls=%async_computation.18 | async-start | bytes 2621440 | tf_op jit(solution)/shard_map/reduce_scatter | solution.py:235
  378.6 5.5 copy-start.8
  378.6 5.5 copy-start.47
  384.1 21.9 %copy-start.23 = (bf16[2,512,4,64]{3,1,2,0:T(8,128)(2,1)S(1)}, bf16[2,512,4,64]{3,1,2,0:T(8,128)(2,1)}, u32[]{:S(2)}) copy-start(bf16[2,512,4,64]{3,1,2,0:T(8,128)(2,1)} %copy.225) | copy-start | bytes 1572868
  384.1 21.9 %copy-start.24 = (bf16[2,512,4,64]{3,1,2,0:T(8,128)(2,1)S(1)}, bf16[2,512,4,64]{3,1,2,0:T(8,128)(2,1)}, u32[]{:S(2)}) copy-start(bf16[2,512,4,64]{3,1,2,0:T(8,128)(2,1)} %copy.226) | copy-start | bytes 1572868
  417.7 19.1 %copy-start.54 = (bf16[2,512,2,2,128]{1,4,3,2,0:T(8,128)(2,1)S(1)}, bf16[2,512,2,2,128]{1,4,3,2,0:T(8,128)(2,1)}, u32[]{:S(2)}) copy-start(bf16[2,512,2,2,128]{1,4,3,2,0:T(8,128)(2,1)} %copy-done.53) | copy-start | bytes 3145732
  417.7 89.6 %reduce-scatter.12.cloned.1.call-start = ((), (), s32[]{:S(2)}) async-start(), calls=%async_computation.19 | async-start | bytes 2621440 | tf_op jit(solution)/shard_map/reduce_scatter | solution.py:238
  436.8 92.2 %reduce-scatter.20.cloned.1.call-start = ((), (), s32[]{:S(2)}) async-start(), calls=%async_computation.23 | async-start | bytes 1572864 | tf_op jit(solution)/shard_map/reduce_scatter | solution.py:299
  443.5 114.5 %reduce-scatter.22.cloned.1.call-start = ((), (), s32[]{:S(2)}) async-start(), calls=%async_computation.24 | async-start | bytes 2359296 | tf_op jit(solution)/shard_map/reduce_scatter | solution.py:305
  448.7 5.4 copy-start.42
  448.7 138.2 %reduce-scatter.24.cloned.1.call-start = ((), (), s32[]{:S(2)}) async-start(), calls=%async_computation.25 | async-start | bytes 2359296 | tf_op jit(solution)/shard_map/reduce_scatter | solution.py:308
  453.9 155.5 %reduce-scatter.14.cloned.1.call-start = ((), (), s32[]{:S(2)}) async-start(), calls=%async_computation.20 | async-start | bytes 1572864 | tf_op jit(solution)/shard_map/reduce_scatter | solution.py:284
  454.1 9.1 copy-start.11
  454.1 9.1 copy-start.15
  469.9 167.7 %reduce-scatter.26.cloned.1.call-start = ((), (), s32[]{:S(2)}) async-start(), calls=%async_computation.26 | async-start | bytes 2359296 | tf_op jit(solution)/shard_map/reduce_scatter | solution.py:311
  470.0 6.3 copy-start.44
  475.2 179.8 %reduce-scatter.16.cloned.1.call-start = ((), (), s32[]{:S(2)}) async-start(), calls=%async_computation.21 | async-start | bytes 786432 | tf_op jit(solution)/shard_map/reduce_scatter | solution.py:287
  486.5 185.8 %reduce-scatter.18.cloned.1.call-start = ((), (), s32[]{:S(2)}) async-start(), calls=%async_computation.22 | async-start | bytes 786432 | tf_op jit(solution)/shard_map/reduce_scatter | solution.py:290
  510.2 250.7 %all-reduce.21.cloned.1.call-start = ((), (), s32[]{:S(2)}) async-start(), calls=%async_computation.27 | async-start | bytes 8388608 | tf_op jit(solution)/shard_map/psum | solution.py:162
  516.4 394.5 %all-reduce.23.cloned.1.call-start = ((), (), s32[]{:S(2)}) async-start(), calls=%async_computation.28 | async-start | bytes 7864320 | tf_op jit(solution)/shard_map/psum | solution.py:317
  910.8 4.9 copy-start.25
  910.8 6.3 copy-start.28
  (30 other events, 66.8 us)
Sparse Core Ops, SparseCore 0:
  10.1 26.9 all-gather.13
  51.8 47.4 all-gather.11
  101.4 44.4 all-gather.9
  147.3 20.0 all-gather.15
  171.4 51.3 all-reduce.16
  224.2 27.2 all-gather.19
  253.1 27.1 all-gather.17
  281.8 27.1 all-gather.21
  322.9 51.3 all-reduce.18
  417.9 43.6 reduce-scatter.9
  464.5 42.8 reduce-scatter.11
  509.4 19.5 reduce-scatter.19
  531.8 26.1 reduce-scatter.21
  560.7 26.1 reduce-scatter.23
  589.0 20.3 reduce-scatter.13
  611.5 26.1 reduce-scatter.25
  640.3 14.6 reduce-scatter.15
  657.7 14.6 reduce-scatter.17
  675.3 85.5 all-reduce.20
  763.7 147.0 all-reduce.22
where the time goes:
time: 935 us; the launch traced here: 928 us
  waiting for transfers between devices  583 us (62%)
  matrix products  173 us (19%)
  other arithmetic  69.9 us (7%)
  blocking collectives  58.7 us (6%)
  local copies, waits for them, and re-layouts  24.3 us (3%)
  between operations  17.4 us (2%)
    psum x1, waiting for transfers between devices, body(): lax.psum(reduced[1].astype(jnp.bfloat16), 'ctx').astype(jnp.float32)  113 us
    psum x1, waiting for transfers between devices, body(): ffn_out = lax.psum(ffn_part.astype(jnp.bfloat16), 'tp').astype(jnp.float32)  87.2 us
    psum x1, waiting for transfers between devices, body(): lax.psum(grad_two_part.astype(jnp.bfloat16), 'tp').astype(jnp.float32)  51.5 us
    psum x1, waiting for transfers between devices, body(): lax.psum(branch_part.astype(jnp.bfloat16), 'tp').astype(jnp.float32)  45 us
    reduce_scatter x1, waiting for transfers between devices, body(): lax.psum_scatter(gate_grad.astype(jnp.bfloat16), 'fsdp', scatter_dimensio...  29 us
    reduce_scatter x1, waiting for transfers between devices, body(): lax.psum_scatter(up_grad.astype(jnp.bfloat16), 'fsdp', scatter_dimension=...  28.9 us
    reduce_scatter x1, waiting for transfers between devices, body(): lax.psum_scatter(down_grad.astype(jnp.bfloat16), 'fsdp', scatter_dimensio...  28.3 us
    all_gather x1, waiting for transfers between devices, body(): piece_keys = lax.all_gather(keys, 'ctx', axis=1, tiled=True)  24.4 us
  transfers between devices with their start and end apart: 20, of which 18 were waited for; matrix products, arithmetic and copies ran while one was open for 20% of the time, Pallas kernels for 0%

commit v1 on v0

--- a/solution.py
+++ b/solution.py
@@ -124,7 +124,24 @@
 
     stat_shape = (seq_count, local_len, kv_local, group_size)
     run_max = jnp.full(stat_shape, masked_score, jnp.float32)
-    piece_keys = lax.all_gather(keys, "ctx", axis=1, tiled=True)
+    size, index, span = (lax.axis_size("ctx"), lax.axis_index("ctx"), keys.shape[1])
+    right = [(i, (i + 1) % size) for i in range(size)]
+    left = [(i, (i - 1) % size) for i in range(size)]
+    whole = jnp.zeros((*keys.shape[:1], size * span, *keys.shape[1 + 1 :]), keys.dtype)
+    whole = lax.dynamic_update_slice_in_dim(whole, keys, index * span, axis=1)
+    from_left = from_right = keys
+    half = size // 2
+    for step in range(1, half + 1):
+        from_left = lax.ppermute(from_left, "ctx", right)
+        whole = lax.dynamic_update_slice_in_dim(
+            whole, from_left, (index - step) % size * span, axis=1
+        )
+        if step < size - half:
+            from_right = lax.ppermute(from_right, "ctx", left)
+            whole = lax.dynamic_update_slice_in_dim(
+                whole, from_right, (index + step) % size * span, axis=1
+            )
+    piece_keys = whole
     piece_values = lax.all_gather(values, "ctx", axis=1, tiled=True)
     allowed = allowed_mask(piece_keys.shape[1])
     scores = (

time: 935 us -> 965 us (1.032)
  matrix products: 173 us -> 192 us
    ppermute x0 -> x3, waiting for transfers between devices: none -> 40.7 us  [the longest x2 40.7 us: body(): from_left = lax.ppermute(from_left, 'ctx', right)]
    dot_general x1 -> x2, matrix products: 16.5 us -> 34.6 us  [body(): jnp.einsum('bqkgd,btkd->bqkgt', queries, piece_keys, preferred_element_ty...]
    reduce_scatter x1, waiting for transfers between devices: 28.3 us -> 11.2 us  [body(): lax.psum_scatter(down_grad.astype(jnp.bfloat16), 'fsdp', scatter_dimensio...]
    psum x1, waiting for transfers between devices: 51.5 us -> 35.1 us  [body(): lax.psum(grad_two_part.astype(jnp.bfloat16), 'tp').astype(jnp.float32)]
    reduce_scatter x1, waiting for transfers between devices: 15.5 us -> 0.01 us  [body(): lax.psum_scatter(value_full.astype(jnp.bfloat16), 'ctx', scatter_dimensio...]
    all_gather x1, waiting for transfers between devices: 15 us -> 0.02 us  [body(): piece_values = lax.all_gather(values, 'ctx', axis=1, tiled=True)]
    reduce_scatter x1, waiting for transfers between devices: 12.6 us -> 22.5 us  [body(): lax.psum_scatter(out_weight_grad.astype(jnp.bfloat16), 'fsdp', scatter_di...]
  transfers between devices with their start and end apart: 20 -> 23, of which waited for: 18 -> 17; matrix products, arithmetic and copies ran while one was open for 20% -> 25% of each run, Pallas kernels for 0% -> 0%
where the time goes in v1:
time: 965 us; the launch traced here: 956 us
  waiting for transfers between devices  583 us (60%)
  matrix products  192 us (20%)
  other arithmetic  69.3 us (7%)
  blocking collectives  58.4 us (6%)
  local copies, waits for them, and re-layouts  30.3 us (3%)
  between operations  17.4 us (2%)
    psum x1, waiting for transfers between devices, body(): lax.psum(reduced[1].astype(jnp.bfloat16), 'ctx').astype(jnp.float32)  112 us
    psum x1, waiting for transfers between devices, body(): ffn_out = lax.psum(ffn_part.astype(jnp.bfloat16), 'tp').astype(jnp.float32)  87.2 us
    psum x1, waiting for transfers between devices, body(): lax.psum(branch_part.astype(jnp.bfloat16), 'tp').astype(jnp.float32)  46.2 us
    ppermute x2, waiting for transfers between devices, body(): from_left = lax.ppermute(from_left, 'ctx', right)  40.7 us
    psum x1, waiting for transfers between devices, body(): lax.psum(grad_two_part.astype(jnp.bfloat16), 'tp').astype(jnp.float32)  35.1 us
    dot_general x2, matrix products, body(): jnp.einsum('bqkgd,btkd->bqkgt', queries, piece_keys, preferred_element_ty...  34.6 us
    all_gather x1, waiting for transfers between devices, body(): piece_keys = lax.all_gather(keys, 'ctx', axis=1, tiled=True)  33.8 us
    reduce_scatter x1, waiting for transfers between devices, body(): lax.psum_scatter(gate_grad.astype(jnp.bfloat16), 'fsdp', scatter_dimensio...  29 us
  transfers between devices with their start and end apart: 23, of which 17 were waited for; matrix products, arithmetic and copies ran while one was open for 25% of the time, Pallas kernels for 0%

profile of v1, /device:TPU:0, one launch (start us, length us, event | category | flops | bytes accessed | tf_op | source)
XLA Modules:
  0.0 955.8 jit_solution(9258555851113935541)
XLA Ops:
  10.2 5.3 all-gather
  16.6 12.6 %all_gather.48 = bf16[1024,256]{0,1:T(8,128)(2,1)S(1)} all-gather(bf16[512,256]{0,1:T(8,128)(2,1)S(1)} %copy.219), channel_id=1, replica_groups=mesh['fsdp'=2,'ctx'=4,'tp'=4] {'fsdp'}, dimensions={0}, use_global_device_ids=true | all-gather | bytes 786432 | tf_op jit(solution)/shard_map/all_gather | solution.py:61
  33.2 5.4 all-reduce.11
  43.7 7.0 all_gather.50
  59.7 3.6 collective-permute-start.1
  64.4 3.8 and_and_fusion
  68.2 40.7 %collective-permute-done = bf16[2,512,2,128]{3,1,2,0:T(8,128)(2,1)} collective-permute-done((bf16[2,512,2,128]{3,1,2,0:T(8,128)(2,1)}, bf16[2,512,2,128]{3,1,2,0:T(8,128)(2,1)}, u32[]{:S(2)}, u32[]{:S(2)}) %collective-permute-start) | collective-permute-done | bytes 524320 | tf_op jit(solution)/shard_map/ppermute | solution.py:135
  123.8 16.6 %fusion.5 = (f32[2,512,2,2]{1,3,2,0:T(2,128)S(1)}, f32[2,2,2048,512,2]{3,2,4,1,0:T(8,128)}) fusion(pred[2,512,2048]{1,2,0:T(8,128)(4,1)} %and_and_fusion, bf16[2,512,2,2,64]{4,1,3,2,0:T(8,128)(2,1)} %bitcast.297, bf16[2,512,2,2,64]{4,1,3,2,0:T(8,128)(2,1)S(1)} %bitcast.294, bf16[2,2048,2,128]{3,1,2,0:T(8,128)(2,1)} %constant_dynamic-update-slice_fusion), kind=kOutput, calls=%fused_computation.9 | convolution fusion | flops 2174742528 | bytes 38813696 | tf_op jit(solution)/shard_map/bqkgd,btkd->bqkgt/dot_general | solution.py:148
  140.4 14.9 %fusion.6 = f32[2,512,2,2]{1,3,2,0:T(2,128)S(1)} fusion(f32[2,2,2048,512,2]{3,2,4,1,0:T(8,128)} %get-tuple-element.76, f32[2,512,2,2]{1,3,2,0:T(2,128)S(1)} %broadcast_maximum_fusion, pred[2,512,2048]{1,2,0:T(8,128)(4,1)S(1)} %copy-done.7), kind=kLoop, calls=%fused_computation.10 | loop fusion | flops 41938944 | bytes 35684352 | tf_op jit(solution)/shard_map/reduce_sum | solution.py:154
  155.4 17.2 %fusion.87 = (bf16[2,512,2,2,128]{1,4,3,2,0:T(8,128)(2,1)}, f32[2,2,128,512,2]{3,2,4,1,0:T(8,128)}) fusion(f32[2,512]{1,0:T(2,128)S(1)} %get-tuple-element.44, f32[2,512,2,2]{1,3,2,0:T(2,128)S(1)} %get-tuple-element.41, f32[2,2,2048,512,2]{3,2,4,1,0:T(8,128)} %get-tuple-element.76, f32[2,512,2,2]{1,3,2,0:T(2,128)S(1)} %broadcast_maximum_fusion, ...), kind=kOutput, calls=%fused_computation.146 | convolution fusion | flops 2190999552 | bytes 40931328 | tf_op jit(solution)/shard_map/bqkgt,btkd->bqkgd/dot_general | solution.py:155
  172.7 4.1 bitcast_convert_fusion
  179.6 4.5 all-gather.1
  184.1 46.2 %all-reduce.17.cloned.1.call-done = bf16[2,512,1024]{2,1,0:T(8,128)(2,1)} async-done(((bf16[2,512,1024]{2,1,0:T(8,128)(2,1)}), bf16[2,512,1024]{2,1,0:T(8,128)(2,1)}) %all-reduce.17.cloned.1.call-update) | async-done | bytes 2097168 | tf_op jit(solution)/shard_map/psum | solution.py:169
  235.3 23.7 %all-gather.18.cloned.1.call-done = bf16[1024,768]{1,0:T(8,128)(2,1)} async-done(((bf16[512,768]{1,0:T(8,128)(2,1)}), bf16[1024,768]{1,0:T(8,128)(2,1)}) %all-gather.18.cloned.1.call-update) | async-done | bytes 1572880 | tf_op jit(solution)/shard_map/all_gather | solution.py:67
  259.0 5.5 fusion.68
  264.4 23.2 %all-gather.16.cloned.1.call-done = bf16[1024,768]{1,0:T(8,128)(2,1)} async-done(((bf16[512,768]{1,0:T(8,128)(2,1)}), bf16[1024,768]{1,0:T(8,128)(2,1)}) %all-gather.16.cloned.1.call-update) | async-done | bytes 1572880 | tf_op jit(solution)/shard_map/all_gather | solution.py:66
  287.6 5.5 fusion.72
  293.1 23.3 %all-gather.20.cloned.1.call-done = bf16[768,1024]{1,0:T(8,128)(2,1)} async-done(((bf16[768,512]{1,0:T(8,128)(2,1)}), bf16[768,1024]{1,0:T(8,128)(2,1)}) %all-gather.20.cloned.1.call-update) | async-done | bytes 1572880 | tf_op jit(solution)/shard_map/all_gather | solution.py:68
  316.4 8.0 multiply_convert_fusion.2
  330.4 33.8 %all-gather.22.cloned.1.call-done = bf16[2,2048,2,128]{3,1,2,0:T(8,128)(2,1)} async-done(((bf16[2,512,2,128]{3,1,2,0:T(8,128)(2,1)}), bf16[2,2048,2,128]{3,1,2,0:T(8,128)(2,1)}) %all-gather.22.cloned.1.call-update) | async-done | bytes 2097168 | tf_op jit(solution)/shard_map/all_gather | solution.py:217
  364.2 18.0 %fusion.46 = f32[2,2,2048,512,2]{3,2,4,1,0:T(8,128)} fusion(bf16[2,2048,2,128]{3,1,2,0:T(8,128)(2,1)} %all-gather.22.cloned.1.call-done, bf16[2,512,2,2,64]{4,1,3,2,0:T(8,128)(2,1)} %bitcast.298, bf16[2,512,2,2,64]{4,1,3,2,0:T(8,128)(2,1)S(1)} %bitcast.295), kind=kOutput, calls=%fused_computation.83 | convolution fusion | flops 2149580800 | bytes 36700160 | tf_op jit(solution)/shard_map/bqkgd,btkd->bqkgt/dot_general | solution.py:222
  382.2 35.1 %all-reduce.19.cloned.1.call-done = bf16[2,512,1024]{2,1,0:T(8,128)(2,1)} async-done(((bf16[2,512,1024]{2,1,0:T(8,128)(2,1)}), bf16[2,512,1024]{2,1,0:T(8,128)(2,1)}) %all-reduce.19.cloned.1.call-update) | async-done | bytes 2097168 | tf_op jit(solution)/shard_map/psum | solution.py:205
  417.4 4.0 fusion.29
  421.5 5.6 multiply_reduce_fusion.2
  427.1 18.3 %fusion.39 = bf16[2,2048,2,128]{1,3,2,0:T(8,128)(2,1)} fusion(bf16[2,512,2,2,128]{1,4,3,2,0:T(8,128)(2,1)} %get-tuple-element.80, f32[2,2,2048,512,2]{3,2,4,1,0:T(8,128)} %fusion.46, f32[2,512,2,2]{1,3,2,0:T(2,128)S(1)} %get-tuple-element.40, pred[2,512,2048]{1,2,0:T(8,128)(4,1)} %and_and_fusion), kind=kOutput, calls=%fused_computation.77 | convolution fusion | flops 2198863872 | bytes 38813696 | tf_op jit(solution)/shard_map/bqkgt,bqkgd->btkd/dot_general | solution.py:230
  445.4 22.8 %fusion.1 = bf16[2,512,2,2,2048]{1,4,3,2,0:T(8,128)(2,1)} fusion(f32[2,2,2048,512,2]{3,2,4,1,0:T(8,128)} %fusion.46, f32[2,512,2,2]{1,3,2,0:T(2,128)S(1)} %get-tuple-element.79, f32[2,512,2,2]{1,3,2,0:T(2,128)S(1)} %get-tuple-element.40, pred[2,512,2048]{1,2,0:T(8,128)(4,1)} %and_and_fusion, bf16[2,512,2,2,128]{1,4,3,2,0:T(8,128)(2,1)} %get-tuple-element.80, ...), kind=kOutput, calls=%fused_computation.2 | convolution fusion | flops 2214592512 | bytes 55607296 | tf_op jit(solution)/shard_map/bqkgd,btkd->bqkgt/dot_general | solution.py:236
  468.2 11.9 %fusion.38 = bf16[2,2048,2,128]{3,1,2,0:T(8,128)(2,1)} fusion(bf16[2,512,2,2,2048]{1,4,3,2,0:T(8,128)(2,1)} %fusion.1, bf16[2,512,2,2,64]{4,1,3,2,0:T(8,128)(2,1)S(1)} %bitcast.299, bf16[2,512,2,2,64]{4,1,3,2,0:T(8,128)(2,1)S(1)} %bitcast.296), kind=kOutput, calls=%fused_computation.76 | convolution fusion | flops 2151677952 | bytes 19922944 | tf_op jit(solution)/shard_map/bqkgt,bqkgd->btkd/dot_general | solution.py:245
  480.1 5.2 bitcast_convert_fusion.2
  485.4 5.1 bitcast_convert_fusion.4
  490.7 5.1 bitcast_convert_fusion.3
  496.0 5.8 fusion.50
  503.0 9.1 fusion.62
  520.1 5.0 convolution_convert_fusion
  528.0 6.3 reduce-scatter.10.cloned.1.call-done
  550.7 11.2 %reduce-scatter.26.cloned.1.call-done = bf16[768,512]{1,0:T(8,128)(2,1)} async-done(((bf16[768,1024]{1,0:T(8,128)(2,1)}), bf16[768,512]{1,0:T(8,128)(2,1)}) %reduce-scatter.26.cloned.1.call-update) | async-done | bytes 786448 | tf_op jit(solution)/shard_map/reduce_scatter | solution.py:328
  561.8 29.0 %reduce-scatter.22.cloned.1.call-done = bf16[512,768]{1,0:T(8,128)(2,1)} async-done(((bf16[1024,768]{1,0:T(8,128)(2,1)}), bf16[512,768]{1,0:T(8,128)(2,1)}) %reduce-scatter.22.cloned.1.call-update) | async-done | bytes 786448 | tf_op jit(solution)/shard_map/reduce_scatter | solution.py:322
  590.8 28.9 %reduce-scatter.24.cloned.1.call-done = bf16[512,768]{1,0:T(8,128)(2,1)} async-done(((bf16[1024,768]{1,0:T(8,128)(2,1)}), bf16[512,768]{1,0:T(8,128)(2,1)}) %reduce-scatter.24.cloned.1.call-update) | async-done | bytes 786448 | tf_op jit(solution)/shard_map/reduce_scatter | solution.py:325
  619.7 22.5 %reduce-scatter.20.cloned.1.call-done = bf16[512,512]{1,0:T(8,128)(2,1)} async-done(((bf16[512,1024]{1,0:T(8,128)(2,1)}), bf16[512,512]{1,0:T(8,128)(2,1)}) %reduce-scatter.20.cloned.1.call-update) | async-done | bytes 524304 | tf_op jit(solution)/shard_map/reduce_scatter | solution.py:316
  642.2 22.5 %reduce-scatter.14.cloned.1.call-done = bf16[512,512]{1,0:T(8,128)(2,1)} async-done(((bf16[1024,512]{1,0:T(8,128)(2,1)}), bf16[512,512]{1,0:T(8,128)(2,1)}) %reduce-scatter.14.cloned.1.call-update) | async-done | bytes 524304 | tf_op jit(solution)/shard_map/reduce_scatter | solution.py:301
  664.7 17.3 %reduce-scatter.18.cloned.1.call-done = bf16[512,256]{1,0:T(8,128)(2,1)} async-done(((bf16[1024,256]{1,0:T(8,128)(2,1)}), bf16[512,256]{1,0:T(8,128)(2,1)}) %reduce-scatter.18.cloned.1.call-update) | async-done | bytes 262160 | tf_op jit(solution)/shard_map/reduce_scatter | solution.py:307
  682.0 17.3 %reduce-scatter.16.cloned.1.call-done = bf16[512,256]{1,0:T(8,128)(2,1)} async-done(((bf16[1024,256]{1,0:T(8,128)(2,1)}), bf16[512,256]{1,0:T(8,128)(2,1)}) %reduce-scatter.16.cloned.1.call-update) | async-done | bytes 262160 | tf_op jit(solution)/shard_map/reduce_scatter | solution.py:304
  700.7 87.2 %all-reduce.21.cloned.1.call-done = (bf16[2,512,1024]{2,1,0:T(8,128)(2,1)}, bf16[2,512,1024]{2,1,0:T(8,128)(2,1)}) async-done(((bf16[2,512,1024]{2,1,0:T(8,128)(2,1)}, bf16[2,512,1024]{2,1,0:T(8,128)(2,1)}), (bf16[2,512,1024]{2,1,0:T(8,128)(2,1)}, bf16[2,512,1024]{2,1,0:T(8,128)(2,1)})) %all-reduce.21.cloned.1.call-update) | async-done | bytes 4194320 | tf_op jit(solution)/shard_map/psum | solution.py:179
  787.9 3.4 fusion.33
  791.4 5.0 all-reduce.10
  796.7 6.0 all-reduce.6
  802.7 12.6 %all-reduce.8 = (bf16[512]{0:T(512)(128)(2,1)S(1)}, bf16[64]{0:T(256)(128)(2,1)S(1)}, bf16[64]{0:T(256)(128)(2,1)S(1)}, bf16[512]{0:T(512)(128)(2,1)S(1)}) all-reduce(bf16[512]{0:T(512)(128)(2,1)S(1)} %dynamic-slice.3, bf16[64]{0:T(256)(128)(2,1)S(1)} %get-tuple-element.17, ...), channel_id=1, replica_groups=mesh['fsdp'=2,'ctx'=4,'tp'=4] {'ctx'}, use_global_device_ids=true, to_apply=%region_21.22 | all-reduce | flops 1152 | bytes 4608 | tf_op jit(solution)/shard_map/psum | solution.py:333
  817.4 8.0 fusion.24
  825.5 112.4 %all-reduce.23.cloned.1.call-done = (bf16[512,512]{1,0:T(8,128)(2,1)}, bf16[512,256]{1,0:T(8,128)(2,1)}, bf16[512,256]{1,0:T(8,128)(2,1)}, bf16[512,512]{1,0:T(8...) async-done(((bf16[512,512]{1,0:T(8,128)(2,1)}, bf16[512,256]{1,0:T(8,128)(2,1)}, bf16[512,256]{1,0:T(8,128)(2,1)}, ...) | async-done | bytes 3932176 | tf_op jit(solution)/shard_map/psum | solution.py:334
  (248 shorter events, 93.1 us)
Async XLA Ops:
  7.2 22.0 %copy-start = (bf16[2,512,1024]{2,1,0:T(8,128)(2,1)S(1)}, bf16[2,512,1024]{2,1,0:T(8,128)(2,1)}, u32[]{:S(2)}) copy-start(bf16[2,512,1024]{2,1,0:T(8,128)(2,1)} %param.14) | copy-start | bytes 6291460
  7.2 105.6 %all-gather.12.cloned.1.call-start = ((), (), s32[]{:S(2)}) async-start(), calls=%async_computation.10 | async-start | bytes 1572864 | tf_op jit(solution)/shard_map/all_gather | solution.py:59
  9.4 146.0 %all-gather.10.cloned.1.call-start = ((), (), s32[]{:S(2)}) async-start(), calls=%async_computation.9 | async-start | bytes 2621440 | tf_op jit(solution)/shard_map/all_gather | solution.py:145
  15.5 97.3 %copy-start.35 = (f32[2,1,512]{2,1,0:T(1,128)}, f32[2,1,512]{2,1,0:T(1,128)S(1)}, u32[]{:S(2)}) copy-start(f32[2,1,512]{2,1,0:T(1,128)S(1)} %convert_element_type.277) | copy-start | bytes 12292
  29.7 8.9 copy-start.29
  29.7 83.1 %copy-start.37 = (f32[2,512]{1,0:T(2,128)}, f32[2,512]{1,0:T(2,128)S(1)}, u32[]{:S(2)}) copy-start(f32[2,512]{1,0:T(2,128)S(1)} %add_rsqrt_fusion.3) | copy-start | bytes 12292
  29.7 10.0 %copy-start.30 = (bf16[512,256]{1,0:T(8,128)(2,1)S(1)}, bf16[512,256]{1,0:T(8,128)(2,1)}, u32[]{:S(2)}) copy-start(bf16[512,256]{1,0:T(8,128)(2,1)} %param.18) | copy-start | bytes 786436
  31.4 141.3 %all-gather.14.cloned.1.call-start = ((), (), s32[]{:S(2)}) async-start(), calls=%async_computation.11 | async-start | bytes 1572864 | tf_op jit(solution)/shard_map/all_gather | solution.py:64
  38.5 15.6 %copy-start.41 = (f32[128]{0:T(128)}, f32[128]{0:T(128)S(1)}, u32[]{:S(2)}) copy-start(f32[128]{0:T(128)S(1)} %convert_element_type.221) | copy-start | bytes 1540
  41.7 10.9 %copy-start.14 = (f32[2,512,64]{1,2,0:T(8,128)}, f32[2,512,64]{1,2,0:T(8,128)S(1)}, u32[]{:S(2)}) copy-start(f32[2,512,64]{1,2,0:T(8,128)S(1)} %get-tuple-element.67) | copy-start | bytes 786436
  41.7 74.3 %copy-start.9 = (f32[2,512,64]{1,2,0:T(8,128)}, f32[2,512,64]{1,2,0:T(8,128)S(1)}, u32[]{:S(2)}) copy-start(f32[2,512,64]{1,2,0:T(8,128)S(1)} %get-tuple-element.68) | copy-start | bytes 786436
  59.7 51.1 %collective-permute-start.1 = (bf16[2,512,2,128]{3,1,2,0:T(8,128)(2,1)}, bf16[2,512,2,128]{3,1,2,0:T(8,128)(2,1)}, u32[]{:S(2)}, u32[]{:S(2)}) collective-permute-start(bf16[2,512,2,128]{3,1,2,0:T(8,128)(2,1)} %get-tuple-element.43), channel_id=1, source_target_pairs={{0,12},{4,0},{8,4},{12,8},{1,13},{5,1},{9,5},{13,9},{2,14},{6,2},{... | collective-permute-start | bytes 1572872 | tf_op jit(solution)/shard_map/ppermute | solution.py:140
  63.4 45.5 %collective-permute-start = (bf16[2,512,2,128]{3,1,2,0:T(8,128)(2,1)}, bf16[2,512,2,128]{3,1,2,0:T(8,128)(2,1)}, u32[]{:S(2)}, u32[]{:S(2)}) collective-permute-start(bf16[2,512,2,128]{3,1,2,0:T(8,128)(2,1)} %get-tuple-element.43), channel_id=1, source_target_pairs={{0,4},{4,8},{8,12},{12,0},{1,5},{5,9},{9,13},{13,1},{2,6},{6,10},{... | collective-permute-start | bytes 1572872 | tf_op jit(solution)/shard_map/ppermute | solution.py:135
  63.4 166.9 %all-reduce.17.cloned.1.call-start = ((), (), s32[]{:S(2)}) async-start(), calls=%async_computation.12 | async-start | bytes 4194304 | tf_op jit(solution)/shard_map/psum | solution.py:169
  63.6 51.9 %copy-start.39 = (f32[128]{0:T(128)}, f32[128]{0:T(128)S(1)}, u32[]{:S(2)}) copy-start(f32[128]{0:T(128)S(1)} %convert_element_type.223) | copy-start | bytes 1540
  108.9 13.0 %collective-permute-start.2 = (bf16[2,512,2,128]{3,1,2,0:T(8,128)(2,1)}, bf16[2,512,2,128]{3,1,2,0:T(8,128)(2,1)}, u32[]{:S(2)}, u32[]{:S(2)}) collective-permute-start(bf16[2,512,2,128]{3,1,2,0:T(8,128)(2,1)} %collective-permute-done), channel_id=1, source_target_pairs={{0,4},{4,8},{8,12},{12,0},{1,5},{5,9},{9,13},{13,1},{2,6},{6,10},{... | collective-permute-start | bytes 1572872 | tf_op jit(solution)/shard_map/ppermute | solution.py:135
  123.8 16.6 %copy-start.7 = (pred[2,512,2048]{1,2,0:T(8,128)(4,1)S(1)}, pred[2,512,2048]{1,2,0:T(8,128)(4,1)}, u32[]{:S(2)}) copy-start(pred[2,512,2048]{1,2,0:T(8,128)(4,1)} %and_and_fusion) | copy-start | bytes 6291460
  176.8 82.1 %all-gather.18.cloned.1.call-start = ((), (), s32[]{:S(2)}) async-start(), calls=%async_computation.14 | async-start | bytes 2359296 | tf_op jit(solution)/shard_map/all_gather | solution.py:67
  177.4 110.2 %all-gather.16.cloned.1.call-start = ((), (), s32[]{:S(2)}) async-start(), calls=%async_computation.13 | async-start | bytes 2359296 | tf_op jit(solution)/shard_map/all_gather | solution.py:66
  178.0 138.4 %all-gather.20.cloned.1.call-start = ((), (), s32[]{:S(2)}) async-start(), calls=%async_computation.15 | async-start | bytes 2359296 | tf_op jit(solution)/shard_map/all_gather | solution.py:68
  178.8 185.4 %all-gather.22.cloned.1.call-start = ((), (), s32[]{:S(2)}) async-start(), calls=%async_computation.17 | async-start | bytes 2621440 | tf_op jit(solution)/shard_map/all_gather | solution.py:217
  179.5 237.9 %all-reduce.19.cloned.1.call-start = ((), (), s32[]{:S(2)}) async-start(), calls=%async_computation.16 | async-start | bytes 4194304 | tf_op jit(solution)/shard_map/psum | solution.py:205
  316.4 8.0 copy-start.46
  330.2 194.9 %reduce-scatter.12.cloned.1.call-start = ((), (), s32[]{:S(2)}) async-start(), calls=%async_computation.19 | async-start | bytes 2621440 | tf_op jit(solution)/shard_map/reduce_scatter | solution.py:255
  417.4 4.0 copy-start.2
  417.4 4.1 copy-start.8
  417.4 4.1 copy-start.22
  445.3 89.0 %reduce-scatter.10.cloned.1.call-start = ((), (), s32[]{:S(2)}) async-start(), calls=%async_computation.18 | async-start | bytes 2621440 | tf_op jit(solution)/shard_map/reduce_scatter | solution.py:252
  445.4 22.8 %copy-start.11 = (bf16[2,512,4,64]{3,1,2,0:T(8,128)(2,1)S(1)}, bf16[2,512,4,64]{3,1,2,0:T(8,128)(2,1)}, u32[]{:S(2)}) copy-start(bf16[2,512,4,64]{3,1,2,0:T(8,128)(2,1)} %copy.226) | copy-start | bytes 1572868
  480.0 81.8 %reduce-scatter.26.cloned.1.call-start = ((), (), s32[]{:S(2)}) async-start(), calls=%async_computation.26 | async-start | bytes 2359296 | tf_op jit(solution)/shard_map/reduce_scatter | solution.py:328
  485.3 105.5 %reduce-scatter.22.cloned.1.call-start = ((), (), s32[]{:S(2)}) async-start(), calls=%async_computation.24 | async-start | bytes 2359296 | tf_op jit(solution)/shard_map/reduce_scatter | solution.py:322
  490.5 5.4 copy-start.40
  490.5 5.5 copy-start.49
  490.5 129.2 %reduce-scatter.24.cloned.1.call-start = ((), (), s32[]{:S(2)}) async-start(), calls=%async_computation.25 | async-start | bytes 2359296 | tf_op jit(solution)/shard_map/reduce_scatter | solution.py:325
  495.9 146.3 %reduce-scatter.20.cloned.1.call-start = ((), (), s32[]{:S(2)}) async-start(), calls=%async_computation.23 | async-start | bytes 1572864 | tf_op jit(solution)/shard_map/reduce_scatter | solution.py:316
  502.9 9.2 copy-start.10
  502.9 9.2 copy-start.16
  502.9 161.8 %reduce-scatter.14.cloned.1.call-start = ((), (), s32[]{:S(2)}) async-start(), calls=%async_computation.20 | async-start | bytes 1572864 | tf_op jit(solution)/shard_map/reduce_scatter | solution.py:301
  516.2 3.9 copy-start.42
  518.8 163.2 %reduce-scatter.18.cloned.1.call-start = ((), (), s32[]{:S(2)}) async-start(), calls=%async_computation.22 | async-start | bytes 786432 | tf_op jit(solution)/shard_map/reduce_scatter | solution.py:307
  528.0 9.0 copy-start.6
  528.0 171.4 %reduce-scatter.16.cloned.1.call-start = ((), (), s32[]{:S(2)}) async-start(), calls=%async_computation.21 | async-start | bytes 786432 | tf_op jit(solution)/shard_map/reduce_scatter | solution.py:304
  544.5 243.5 %all-reduce.21.cloned.1.call-start = ((), (), s32[]{:S(2)}) async-start(), calls=%async_computation.27 | async-start | bytes 8388608 | tf_op jit(solution)/shard_map/psum | solution.py:179
  550.6 387.2 %all-reduce.23.cloned.1.call-start = ((), (), s32[]{:S(2)}) async-start(), calls=%async_computation.28 | async-start | bytes 7864320 | tf_op jit(solution)/shard_map/psum | solution.py:334
  937.8 5.9 copy-start.28
  937.8 7.0 copy-start.26
  940.1 6.0 copy-start.25
  943.7 3.6 copy-start.24
  (27 other events, 53.2 us)
Sparse Core Ops, SparseCore 0:
  10.1 25.7 all-gather.11
  38.1 70.9 all-gather.9
  110.6 20.4 all-gather.13
  177.0 53.3 all-reduce.16
  231.7 27.2 all-gather.17
  260.4 27.1 all-gather.15
  289.1 27.1 all-gather.19
  318.5 45.6 all-gather.21
  367.1 50.1 all-reduce.18
  445.5 43.6 reduce-scatter.11
  491.5 42.8 reduce-scatter.9
  536.4 25.3 reduce-scatter.25
  564.6 26.1 reduce-scatter.21
  593.5 26.1 reduce-scatter.23
  621.8 20.3 reduce-scatter.19
  644.3 20.3 reduce-scatter.13
  667.3 14.6 reduce-scatter.17
  684.7 14.6 reduce-scatter.15
  702.4 85.5 all-reduce.20
  790.7 147.0 all-reduce.22
